TPU v7x, 32 devices: a whole 2x2x4 slice. The times are simulated.
32 devices in a mesh: ctx: 8 (over y, x, core), fsdp: 4 (over z).
Axes of the slice: x: 2, y: 2, z: 4, core: 2. Of those that a mesh axis runs over, the one named last changes fastest.
Arguments:
- tokens: bfloat16 [4096, 1600], P(('fsdp', 'ctx')), may hold values from -6 to 6
- block_table: int32 [8, 2], replicated, may hold values from 0 to 15, as said below
- ln1_gain: bfloat16 [1600], P('fsdp'), may hold values from 0.099609375 to 1.8984375
- ln1_bias: bfloat16 [1600], P('fsdp'), may hold values from -1.75 to 1.75
- qkv_weight: bfloat16 [1600, 4800], P('fsdp'), may hold values from -0.15625 to 0.15625
- query_bias: bfloat16 [1600], P('fsdp'), may hold values from -3 to 3
- value_bias: bfloat16 [1600], P('fsdp'), may hold values from -0.875 to 0.875
- proj_weight: bfloat16 [1600, 1600], P('fsdp'), may hold values from -1.25 to 1.25
- proj_bias: bfloat16 [1600], P('fsdp'), may hold values from -1.75 to 1.75
- ln2_gain: bfloat16 [1600], P('fsdp'), may hold values from 0.099609375 to 1.8984375
- ln2_bias: bfloat16 [1600], P('fsdp'), may hold values from -1.75 to 1.75
- fc_weight: bfloat16 [1600, 6400], P('fsdp'), may hold values from -0.15625 to 0.15625
- fc_bias: bfloat16 [6400], P('fsdp'), may hold values from -3 to 3
- out_weight: bfloat16 [6400, 1600], P('fsdp'), may hold values from -0.078125 to 0.078125
- out_bias: bfloat16 [1600], P('fsdp'), may hold values from -1.75 to 1.75
- cotangent: bfloat16 [4096, 1600], P(('fsdp', 'ctx')), may hold values from -6 to 6
Outputs:
- layer_out: bfloat16 [4096, 1600], P(('fsdp', 'ctx'))
- grad_tokens: bfloat16 [4096, 1600], P(('fsdp', 'ctx'))
- grad_ln1_gain: float32 [1600], P('fsdp')
- grad_ln1_bias: float32 [1600], P('fsdp')
- grad_qkv_weight: float32 [1600, 4800], P('fsdp')
- grad_query_bias: float32 [1600], P('fsdp')
- grad_value_bias: float32 [1600], P('fsdp')
- grad_proj_weight: float32 [1600, 1600], P('fsdp')
- grad_proj_bias: float32 [1600], P('fsdp')
- grad_ln2_gain: float32 [1600], P('fsdp')
- grad_ln2_bias: float32 [1600], P('fsdp')
- grad_fc_weight: float32 [1600, 6400], P('fsdp')
- grad_fc_bias: float32 [6400], P('fsdp')
- grad_out_weight: float32 [6400, 1600], P('fsdp')
- grad_out_bias: float32 [1600], P('fsdp')
Inputs may be any that keep to these rules, and one draw needn't show every extreme that they name: `block_table`: row i is (p_i, 15 - p_i) with p_i below 8; every block number appears exactly once.
All inputs are finite; a program needn't handle non-finite values.
Results may differ from a plain program's by a relative error of at most 0.02.
Values may be sent and summed in bfloat16 or wider, within the bound.
A program may use at most 256 MiB of HBM per device.

v0:
```python
import math
import jax
import jax.numpy as jnp
from jax import lax
from jax.sharding import PartitionSpec as P

HEADS = 25


def layer_norm(values, gain_vec, shift_vec):
    centre = values - jnp.mean(values, axis=-1, keepdims=True)
    spread = jnp.mean(centre * centre, axis=-1, keepdims=True)
    return centre * lax.rsqrt(spread + 1e-05) * gain_vec + shift_vec


def gelu_tanh(values):
    return jax.nn.gelu(values, approximate=True)


def body(
    tokens,
    block_table,
    ln1_gain,
    ln1_bias,
    qkv_weight,
    query_bias,
    value_bias,
    proj_weight,
    proj_bias,
    ln2_gain,
    ln2_bias,
    fc_weight,
    fc_bias,
    out_weight,
    out_bias,
    cotangent,
):
    row_count = tokens.shape[0]
    model_width = tokens.shape[1]
    block_rows = row_count // 2
    head_dim = model_width // HEADS
    score_scale = head_dim ** (-0.5)
    ctx_index = lax.axis_index("ctx")
    own_blocks = lax.dynamic_slice_in_dim(block_table, ctx_index, 1, 0).reshape(-1)
    offsets = jnp.arange(block_rows, dtype=jnp.int32)
    query_pos = (own_blocks[:, None] * block_rows + offsets[None, :]).reshape(-1)
    key_pos = (block_table.reshape(-1)[:, None] * block_rows + offsets[None, :]).reshape(-1)
    seq_len = key_pos.shape[0]
    key_block = math.gcd(seq_len, 512)
    block_count = seq_len // key_block
    pos_blocks = key_pos.reshape(block_count, key_block)
    gain_one, shift_one, qkv_full, q_bias, v_bias, proj_full, proj_b = (
        lax.all_gather(ln1_gain, "fsdp", axis=0, tiled=True),
        lax.all_gather(ln1_bias, "fsdp", axis=0, tiled=True),
        lax.all_gather(qkv_weight, "fsdp", axis=0, tiled=True),
        lax.all_gather(query_bias, "fsdp", axis=0, tiled=True),
        lax.all_gather(value_bias, "fsdp", axis=0, tiled=True),
        lax.all_gather(proj_weight, "fsdp", axis=0, tiled=True),
        lax.all_gather(proj_bias, "fsdp", axis=0, tiled=True),
    )
    inputs = tokens.astype(jnp.float32)
    gain_one_f = gain_one.astype(jnp.float32)
    shift_one_f = shift_one.astype(jnp.float32)
    normed_one = layer_norm(inputs, gain_one_f, shift_one_f).astype(jnp.bfloat16)
    bias_row = jnp.concatenate([q_bias, jnp.zeros_like(q_bias), v_bias]).astype(jnp.float32)
    joined = jnp.dot(normed_one, qkv_full, preferred_element_type=jnp.float32) + bias_row
    query_rows = joined[:, :model_width].astype(jnp.bfloat16).reshape(row_count, HEADS, head_dim)
    key_local = joined[:, model_width : 2 * model_width].astype(jnp.bfloat16)
    value_local = joined[:, 2 * model_width :].astype(jnp.bfloat16)
    key_all, value_all = (
        lax.all_gather(key_local, "ctx", axis=0, tiled=True),
        lax.all_gather(value_local, "ctx", axis=0, tiled=True),
    )

    def scores_of(key_tile, pos_tile):
        raw_scores = jnp.einsum(
            "qhd,khd->hqk", query_rows, key_tile, preferred_element_type=jnp.float32
        )
        allowed = pos_tile[None, :] <= query_pos[:, None]
        return (jnp.where(allowed[None], raw_scores * score_scale, -1e30), allowed)

    key_tiles = key_all.reshape(block_count, key_block, HEADS, head_dim)
    value_tiles = value_all.reshape(block_count, key_block, HEADS, head_dim)

    def stat_step(carried, tile_set):
        top_prev, total_prev = carried
        scores, allowed = scores_of(tile_set[0], tile_set[1])
        top_new = jnp.maximum(top_prev, jnp.max(scores, axis=-1))
        total_new = total_prev * jnp.exp(top_prev - top_new) + jnp.sum(
            jnp.exp(scores - top_new[..., None]), axis=-1
        )
        return ((top_new, total_new), None)

    start_stats = (
        jnp.full((HEADS, row_count), -1e30, jnp.float32),
        jnp.zeros((HEADS, row_count), jnp.float32),
    )
    (top_all, total_all), _ = lax.scan(stat_step, start_stats, (key_tiles, pos_blocks))
    log_total = top_all + jnp.log(total_all)

    def out_step(summed, tile_set):
        scores, allowed = scores_of(tile_set[0], tile_set[2])
        soft_w = jnp.exp(scores - log_total[..., None]).astype(jnp.bfloat16)
        return (
            summed
            + jnp.einsum("hqk,khd->qhd", soft_w, tile_set[1], preferred_element_type=jnp.float32),
            None,
        )

    heads_f, _ = lax.scan(
        out_step,
        jnp.zeros((row_count, HEADS, head_dim), jnp.float32),
        (key_tiles, value_tiles, pos_blocks),
    )
    heads_low = heads_f.reshape(row_count, model_width).astype(jnp.bfloat16)
    middle = (
        inputs
        + jnp.dot(heads_low, proj_full, preferred_element_type=jnp.float32)
        + proj_b.astype(jnp.float32)
    )
    fsdp_count = lax.axis_size("fsdp")
    width_share = model_width // fsdp_count
    small_stack = jnp.stack([ln2_gain, ln2_bias, out_bias], axis=1)
    small_tiled = jnp.tile(small_stack, (1, fsdp_count))
    fc_cols, small_full = (
        lax.all_to_all(fc_weight, "fsdp", split_axis=1, concat_axis=0, tiled=True),
        lax.all_to_all(small_tiled, "fsdp", split_axis=1, concat_axis=0, tiled=True),
    )
    gain_two_f = small_full[:, 0].astype(jnp.float32)
    shift_two_f = small_full[:, 1].astype(jnp.float32)
    out_b_f = small_full[:, 2].astype(jnp.float32)
    normed_two = layer_norm(middle, gain_two_f, shift_two_f).astype(jnp.bfloat16)
    group_normed, group_upstream = (
        lax.all_gather(normed_two, "fsdp", axis=0, tiled=True),
        lax.all_gather(cotangent, "fsdp", axis=0, tiled=True),
    )
    hidden_pre = jnp.dot(
        group_normed, fc_cols, preferred_element_type=jnp.float32
    ) + fc_bias.astype(jnp.float32)
    hidden = gelu_tanh(hidden_pre).astype(jnp.bfloat16)
    rows = hidden
    summed_out = lax.psum_scatter(
        jnp.dot(rows, out_weight, preferred_element_type=jnp.float32).astype(jnp.bfloat16),
        "fsdp",
        scatter_dimension=0,
        tiled=True,
    ).astype(jnp.float32)
    output = middle + summed_out + out_b_f
    out_rows = output.astype(jnp.bfloat16)
    owned_ow = jnp.einsum("tf,td->fd", hidden, group_upstream, preferred_element_type=jnp.float32)
    full_out_b = jnp.sum(group_upstream.astype(jnp.float32), axis=0)
    owned_ob = lax.dynamic_slice_in_dim(
        full_out_b, lax.axis_index("fsdp") * width_share, width_share, 0
    )
    grad_hidden = jnp.einsum(
        "td,fd->tf", group_upstream, out_weight, preferred_element_type=jnp.float32
    )
    _, gelu_pull = jax.vjp(gelu_tanh, hidden_pre)
    grad_pre = gelu_pull(grad_hidden)[0].astype(jnp.bfloat16)
    grad_fc_cols = jnp.einsum(
        "tc,tf->cf", group_normed, grad_pre, preferred_element_type=jnp.float32
    )
    owned_fcb = jnp.sum(grad_pre.astype(jnp.float32), axis=0)
    rows = grad_pre
    grad_normed_two = lax.psum_scatter(
        jnp.einsum("tf,cf->tc", rows, fc_cols, preferred_element_type=jnp.float32).astype(
            jnp.bfloat16
        ),
        "fsdp",
        scatter_dimension=0,
        tiled=True,
    ).astype(jnp.float32)
    _, norm_pull_two = jax.vjp(layer_norm, middle, gain_two_f, shift_two_f)
    grad_mid_norm, grad_gain_two, grad_shift_two = norm_pull_two(grad_normed_two)
    grad_middle = cotangent.astype(jnp.float32) + grad_mid_norm
    norm_pair = jnp.stack([grad_gain_two, grad_shift_two], axis=1)
    owned_fcw, norm_parts = (
        lax.all_to_all(
            grad_fc_cols.astype(jnp.bfloat16), "fsdp", split_axis=0, concat_axis=1, tiled=True
        ).astype(grad_fc_cols.dtype),
        lax.all_to_all(
            norm_pair.astype(jnp.bfloat16), "fsdp", split_axis=0, concat_axis=1, tiled=True
        ).astype(norm_pair.dtype),
    )
    norm_sums = jnp.sum(norm_parts.reshape(width_share, fsdp_count, 2), axis=1)
    owned_g2 = norm_sums[:, 0]
    owned_b2 = norm_sums[:, 1]
    total_g2, total_b2, total_fcw, total_fcb, total_ow, total_ob = (
        lax.psum(owned_g2.astype(jnp.bfloat16), "ctx").astype(jnp.float32),
        lax.psum(owned_b2.astype(jnp.bfloat16), "ctx").astype(jnp.float32),
        lax.psum(owned_fcw.astype(jnp.bfloat16), "ctx").astype(jnp.float32),
        lax.psum(owned_fcb.astype(jnp.bfloat16), "ctx").astype(jnp.float32),
        lax.psum(owned_ow.astype(jnp.bfloat16), "ctx").astype(jnp.float32),
        lax.psum(owned_ob.astype(jnp.bfloat16), "ctx").astype(jnp.float32),
    )
    grad_branch = grad_middle.astype(jnp.bfloat16)
    grad_proj_w = jnp.einsum(
        "tc,td->cd", heads_low, grad_branch, preferred_element_type=jnp.float32
    )
    grad_proj_b = jnp.sum(grad_branch.astype(jnp.float32), axis=0)
    grad_heads = jnp.einsum(
        "td,cd->tc", grad_branch, proj_full, preferred_element_type=jnp.float32
    ).astype(jnp.bfloat16)
    grad_heads_split = grad_heads.reshape(row_count, HEADS, head_dim)
    delta_rows = jnp.sum(grad_heads_split.astype(jnp.float32) * heads_f, axis=-1).T

    def grad_step(grad_query, tile_set):
        key_tile, value_tile, pos_tile = tile_set
        scores, allowed = scores_of(key_tile, pos_tile)
        soft_w = jnp.exp(scores - log_total[..., None])
        grad_soft = jnp.einsum(
            "qhd,khd->hqk", grad_heads_split, value_tile, preferred_element_type=jnp.float32
        )
        grad_raw = jnp.where(
            allowed[None], soft_w * (grad_soft - delta_rows[..., None]) * score_scale, 0.0
        ).astype(jnp.bfloat16)
        grad_query = grad_query + jnp.einsum(
            "hqk,khd->qhd", grad_raw, key_tile, preferred_element_type=jnp.float32
        )
        grad_key = jnp.einsum(
            "hqk,qhd->khd", grad_raw, query_rows, preferred_element_type=jnp.float32
        )
        grad_value = jnp.einsum(
            "hqk,qhd->khd",
            soft_w.astype(jnp.bfloat16),
            grad_heads_split,
            preferred_element_type=jnp.float32,
        )
        return (grad_query, (grad_key, grad_value))

    grad_query, (key_grads, value_grads) = lax.scan(
        grad_step,
        jnp.zeros((row_count, HEADS, head_dim), jnp.float32),
        (key_tiles, value_tiles, pos_blocks),
    )
    key_terms = key_grads.reshape(seq_len, model_width)
    value_terms = value_grads.reshape(seq_len, model_width)
    key_mine, value_mine = (
        lax.psum_scatter(
            key_terms.astype(jnp.bfloat16), "ctx", scatter_dimension=0, tiled=True
        ).astype(jnp.float32),
        lax.psum_scatter(
            value_terms.astype(jnp.bfloat16), "ctx", scatter_dimension=0, tiled=True
        ).astype(jnp.float32),
    )
    grad_joined = jnp.concatenate(
        [grad_query.reshape(row_count, model_width), key_mine, value_mine], axis=1
    ).astype(jnp.bfloat16)
    grad_q_bias = jnp.sum(grad_joined[:, :model_width].astype(jnp.float32), axis=0)
    grad_v_bias = jnp.sum(grad_joined[:, 2 * model_width :].astype(jnp.float32), axis=0)
    grad_qkv_w = jnp.einsum(
        "tc,tk->ck", normed_one, grad_joined, preferred_element_type=jnp.float32
    )
    grad_normed_one = jnp.einsum(
        "tk,ck->tc", grad_joined, qkv_full, preferred_element_type=jnp.float32
    )
    _, norm_pull_one = jax.vjp(layer_norm, inputs, gain_one_f, shift_one_f)
    grad_in_norm, grad_gain_one, grad_shift_one = norm_pull_one(grad_normed_one)
    grad_inputs = (grad_middle + grad_in_norm).astype(jnp.bfloat16)
    owned_g1, owned_b1, owned_qkv, owned_qb, owned_vb, owned_pw, owned_pb = (
        lax.psum_scatter(
            grad_gain_one.astype(jnp.bfloat16), "fsdp", scatter_dimension=0, tiled=True
        ).astype(jnp.float32),
        lax.psum_scatter(
            grad_shift_one.astype(jnp.bfloat16), "fsdp", scatter_dimension=0, tiled=True
        ).astype(jnp.float32),
        lax.psum_scatter(
            grad_qkv_w.astype(jnp.bfloat16), "fsdp", scatter_dimension=0, tiled=True
        ).astype(jnp.float32),
        lax.psum_scatter(
            grad_q_bias.astype(jnp.bfloat16), "fsdp", scatter_dimension=0, tiled=True
        ).astype(jnp.float32),
        lax.psum_scatter(
            grad_v_bias.astype(jnp.bfloat16), "fsdp", scatter_dimension=0, tiled=True
        ).astype(jnp.float32),
        lax.psum_scatter(
            grad_proj_w.astype(jnp.bfloat16), "fsdp", scatter_dimension=0, tiled=True
        ).astype(jnp.float32),
        lax.psum_scatter(
            grad_proj_b.astype(jnp.bfloat16), "fsdp", scatter_dimension=0, tiled=True
        ).astype(jnp.float32),
    )
    total_g1, total_b1, total_qkv, total_qb, total_vb, total_pw, total_pb = (
        lax.psum(owned_g1.astype(jnp.bfloat16), "ctx").astype(jnp.float32),
        lax.psum(owned_b1.astype(jnp.bfloat16), "ctx").astype(jnp.float32),
        lax.psum(owned_qkv.astype(jnp.bfloat16), "ctx").astype(jnp.float32),
        lax.psum(owned_qb.astype(jnp.bfloat16), "ctx").astype(jnp.float32),
        lax.psum(owned_vb.astype(jnp.bfloat16), "ctx").astype(jnp.float32),
        lax.psum(owned_pw.astype(jnp.bfloat16), "ctx").astype(jnp.float32),
        lax.psum(owned_pb.astype(jnp.bfloat16), "ctx").astype(jnp.float32),
    )
    return (
        out_rows,
        grad_inputs,
        total_g1,
        total_b1,
        total_qkv,
        total_qb,
        total_vb,
        total_pw,
        total_pb,
        total_g2,
        total_b2,
        total_fcw,
        total_fcb,
        total_ow,
        total_ob,
    )


def solution(mesh):
    placed = (
        P(("fsdp", "ctx"), None),
        P(),
        P("fsdp"),
        P("fsdp"),
        P("fsdp", None),
        P("fsdp"),
        P("fsdp"),
        P("fsdp", None),
        P("fsdp"),
        P("fsdp"),
        P("fsdp"),
        P("fsdp", None),
        P("fsdp"),
        P("fsdp", None),
        P("fsdp"),
        P(("fsdp", "ctx"), None),
    )
    return jax.shard_map(
        body,
        mesh=mesh,
        in_specs=placed,
        out_specs=(
            P(("fsdp", "ctx"), None),
            P(("fsdp", "ctx"), None),
            P("fsdp"),
            P("fsdp"),
            P("fsdp", None),
            P("fsdp"),
            P("fsdp"),
            P("fsdp", None),
            P("fsdp"),
            P("fsdp"),
            P("fsdp"),
            P("fsdp", None),
            P("fsdp"),
            P("fsdp", None),
            P("fsdp"),
        ),
        check_vma=False,
    )
```

profile of v0, /device:TPU:0, one launch (start us, length us, event | category | flops | bytes accessed | tf_op | source)
XLA Modules:
  0.0 1569.6 jit_solution(5104515425968146760)
XLA Ops:
  10.6 21.1 %all-reduce.13 = (bf16[1600]{0:T(1024)(128)(2,1)S(1)}, bf16[1600]{0:T(1024)(128)(2,1)S(1)}, bf16[1600]{0:T(1024)(128)(2,1)S(1)}, bf16[1600]{0:T(1024)(128)(2,1)S(1)}, bf16[1600]{0:T(1024)(128)(2,1)S(1)}) all-reduce(bf16[1600]{0:T(1024)(128)(2,1)S(1)} %dynamic-update-slice.2, ...), channel_id=1, replica_groups=mesh['ctx'=8,'fsdp'=4] {'fsdp'}, use_global_device_ids=true, to_apply=%add.2 | all-reduce | flops 8000 | bytes 32000
  32.8 246.5 %all-gather.7.cloned.1.call-done = bf16[1600,4800]{1,0:T(8,128)(2,1)} async-done(((bf16[400,4800]{1,0:T(8,128)(2,1)}), bf16[1600,4800]{1,0:T(8,128)(2,1)}) %all-gather.7.cloned.1.call-update) | async-done | bytes 15360016 | tf_op jit(solution)/shard_map/all_gather | solution.py:55
  279.4 12.1 fusion.80
  299.0 11.7 all_to_all.51
  310.7 5.9 copy.78
  316.8 5.1 all-to-all-start.1
  324.4 8.5 reshape.304
  335.8 19.6 %while.39 = (s32[]{:T(128)}, f32[25,128]{1,0:T(8,128)S(1)}, f32[25,128]{1,0:T(8,128)S(1)}, s32[2,512]{1,0:T(2,128)S(1)}, bf16[2,512,25,64]{1,3,2,0:T(8,128)(2,1)...) while((s32[]{:T(128)}, f32[25,128]{1,0:T(8,128)S(1)}, ...), condition=%wide.region_5.6_spmd.clone, body=%wide.region_2.5_spmd.clone.sunk | while | flops 221265664 | bytes 15526528 | solution.py:98
  336.1 5.2 fusion.175
  345.9 5.2 fusion.175
  355.3 4.9 all-gather.9.cloned.1.call-done
  360.2 8.5 reshape.303
  368.7 4.8 copy.75
  373.5 21.0 %while.40 = (s32[]{:T(128)}, f32[128,25,64]{0,2,1:T(8,128)}, bf16[2,512,25,64]{1,3,2,0:T(8,128)(2,1)}, s32[2,512]{1,0:T(2,128)S(1)}, bf16[2,512,25,64]{1,3,2,0:T...) while((s32[]{:T(128)}, f32[128,25,64]{0,2,1:T(8,128)}, ...), condition=%wide.region_7.8_spmd.clone, body=%wide.region_6.7_spmd.clone.sunk | while | flops 426459264 | bytes 5482114 | solution.py:110
  373.8 4.7 fusion.181
  378.8 5.0 fusion.181
  396.5 129.3 %all-gather.13.cloned.1.call-done = bf16[1600,1600]{1,0:T(8,128)(2,1)} async-done(((bf16[400,1600]{1,0:T(8,128)(2,1)}), bf16[1600,1600]{1,0:T(8,128)(2,1)}) %all-gather.13.cloned.1.call-update) | async-done | bytes 5120016 | tf_op jit(solution)/shard_map/all_gather | solution.py:58
  525.8 5.0 fusion.125
  533.0 31.9 %all-gather.17.cloned.1.call-done = bf16[512,1600]{0,1:T(8,128)(2,1)} async-done(((bf16[128,1600]{0,1:T(8,128)(2,1)}), bf16[512,1600]{0,1:T(8,128)(2,1)}) %all-gather.17.cloned.1.call-update) | async-done | bytes 1638416 | tf_op jit(solution)/shard_map/all_gather | solution.py:135
  564.9 7.9 fusion.126
  572.8 31.1 %all-gather.15.cloned.1.call-done = bf16[512,1600]{0,1:T(8,128)(2,1)} async-done(((bf16[128,1600]{0,1:T(8,128)(2,1)}), bf16[512,1600]{0,1:T(8,128)(2,1)}) %all-gather.15.cloned.1.call-update) | async-done | bytes 1638416 | tf_op jit(solution)/shard_map/all_gather | solution.py:134
  603.9 11.7 fusion.118
  616.8 6.7 convolution_convert_fusion.4
  627.1 35.8 %reduce-scatter.21.cloned.1.call-done = bf16[128,1600]{1,0:T(8,128)(2,1)} async-done(((bf16[512,1600]{1,0:T(8,128)(2,1)}), bf16[128,1600]{1,0:T(8,128)(2,1)}) %reduce-scatter.21.cloned.1.call-update) | async-done | bytes 409616
  675.4 49.1 %while.41 = (s32[]{:T(128)}, f32[128,25,64]{0,2,1:T(8,128)}, bf16[2,512,25,64]{1,3,2,0:T(8,128)(2,1)}, bf16[2,512,25,64]{1,3,2,0:T(8,128)(2,1)}, bf16[2,512,25,6...) while((s32[]{:T(128)}, f32[128,25,64]{0,2,1:T(8,128)}, ...), condition=%wide.region_16.17_spmd.clone, body=%wide.region_15.16_spmd.clone.sunk | while | flops 1068712064 | bytes 150980000 | solution.py:231
  675.8 5.2 fusion.192
  681.3 6.4 fusion.193
  700.1 5.1 fusion.192
  705.5 6.4 fusion.193
  724.5 5.3 copy.82
  750.5 30.1 %reduce-scatter.25.cloned.1.call-done = bf16[128,1600]{1,0:T(8,128)(2,1)} async-done(((bf16[1024,1600]{1,0:T(8,128)(2,1)}), bf16[128,1600]{1,0:T(8,128)(2,1)}) %reduce-scatter.25.cloned.1.call-update) | async-done | bytes 409616
  781.9 50.1 %reduce-scatter.23.cloned.1.call-done = bf16[128,1600]{1,0:T(8,128)(2,1)} async-done(((bf16[1024,1600]{1,0:T(8,128)(2,1)}), bf16[128,1600]{1,0:T(8,128)(2,1)}) %reduce-scatter.23.cloned.1.call-update) | async-done | bytes 409616
  833.4 8.5 convolution_convert_fusion
  843.3 6.3 convolution_convert_fusion.2
  849.6 5.1 all-to-all-start.3
  855.0 8.0 convolution_convert_fusion.5
  866.8 8.1 convolution_convert_fusion.1
  874.9 176.1 %all-to-all-done.3 = bf16[4,400,1600]{2,1,0:T(8,128)(2,1)} async-done(((bf16[4,400,1600]{2,1,0:T(8,128)(2,1)}), bf16[4,400,1600]{2,1,0:T(8,128)(2,1)}, u32[]{:S(2)}, u32[]{:S(2)}) %all-to-all-start.3) | async-done | bytes 5120032 | tf_op jit(solution)/shard_map/all_to_all | solution.py:178
  1051.0 6.9 copy.84
  1057.9 9.8 all_to_all.59
  1067.8 228.2 %reduce-scatter.15.cloned.1.call-done = bf16[400,4800]{1,0:T(8,128)(2,1)} async-done(((bf16[1600,4800]{1,0:T(8,128)(2,1)}), bf16[400,4800]{1,0:T(8,128)(2,1)}) %reduce-scatter.15.cloned.1.call-update) | async-done | bytes 3840016 | tf_op jit(solution)/shard_map/reduce_scatter | solution.py:267
  1301.9 33.4 %reduce-scatter.19.cloned.1.call-done = bf16[128,1600]{1,0:T(8,128)(2,1)} async-done(((bf16[512,1600]{1,0:T(8,128)(2,1)}), bf16[128,1600]{1,0:T(8,128)(2,1)}) %reduce-scatter.19.cloned.1.call-update) | async-done | bytes 409616
  1336.7 9.3 fusion.117
  1346.6 16.9 %all-reduce.12 = (bf16[1600]{0:T(1024)(128)(2,1)S(1)}, bf16[1600]{0:T(1024)(128)(2,1)S(1)}, bf16[1600]{0:T(1024)(128)(2,1)S(1)}, bf16[1600]{0:T(1024)(128)(2,1)S(1)}, bf16[1600]{0:T(1024)(128)(2,1)S(1)}) all-reduce(bf16[1600]{0:T(1024)(128)(2,1)S(1)} %get-tuple-element.374, ...), channel_id=6, replica_groups=mesh['ctx'=8,'fsdp'=4] {'fsdp'}, use_global_device_ids=true, to_apply=%region_22.23.clone | all-reduce | flops 8000 | bytes 32000
  1363.9 24.1 %all-reduce.10 = (bf16[400]{0:T(512)(128)(2,1)S(1)}, bf16[400]{0:T(512)(128)(2,1)S(1)}, bf16[400]{0:T(512)(128)(2,1)S(1)}, bf16[400]{0:T(512)(128)(2,1)S(1)}, bf...) all-reduce(bf16[400]{0:T(512)(128)(2,1)S(1)} %dynamic-slice.6, ...), channel_id=1, replica_groups=mesh['ctx'=8,'fsdp'=4] {'ctx'}, use_global_device_ids=true, to_apply=%region_23.24 | all-reduce | flops 4800 | bytes 19200 | tf_op jit(solution)/shard_map/psum | solution.py:284
  1395.2 150.3 %all-reduce.16.cloned.1.call-done = (bf16[400,4800]{1,0:T(8,128)(2,1)}, bf16[400,1600]{1,0:T(8,128)(2,1)}, bf16[400,6400]{1,0:T(8,128)(2,1)}, bf16[1600,1600]{1,0:T(8,128)(2,1)}) async-done(((bf16[400,4800]{1,0:T(8,128)(2,1)}, bf16[400,1600]{1,0:T(8,128)(2,1)}, bf16[400,6400]{1,0:T(8,128)(2,1)}, bf16[1600,1600]{1,0:T(8,128)(2,1)}), (bf16[400,4800]{1,0:T(8,128)(2,1)}, bf16[400,1600]{1,0:T(8,128)(2,1)}, ...) | async-done | bytes 15360016 | tf_op jit(solution)/shard_map/psum | solution.py:286
  1545.5 6.0 convert_element_type.266
  1557.9 4.8 convert_element_type.281
  (307 shorter events, 122.6 us)
Async XLA Ops:
  7.2 24.6 %copy-start.7 = (bf16[128,1600]{0,1:T(8,128)(2,1)S(1)}, bf16[128,1600]{0,1:T(8,128)(2,1)}, u32[]{:S(2)}) copy-start(bf16[128,1600]{0,1:T(8,128)(2,1)} %param.22) | copy-start | bytes 1228804
  7.3 272.1 %all-gather.7.cloned.1.call-start = ((), (), s32[]{:S(2)}) async-start(), calls=%async_computation.10 | async-start | bytes 19456000 | tf_op jit(solution)/shard_map/all_gather | solution.py:55
  8.0 316.4 %all-gather.11.cloned.1.call-start = ((), (), s32[]{:S(2)}) async-start(), calls=%async_computation.12 | async-start | bytes 3686400 | tf_op jit(solution)/shard_map/all_gather | solution.py:71
  31.7 259.8 %copy-start.28 = (f32[1600]{0:T(1024)}, f32[1600]{0:T(1024)S(1)}, u32[]{:S(2)}) copy-start(f32[1600]{0:T(1024)S(1)} %convert_element_type.230) | copy-start | bytes 19204
  31.8 259.7 %copy-start.30 = (f32[1600]{0:T(1024)}, f32[1600]{0:T(1024)S(1)}, u32[]{:S(2)}) copy-start(f32[1600]{0:T(1024)S(1)} %convert_element_type.231) | copy-start | bytes 19204
  32.1 259.4 %copy-start.33 = (f32[128]{0:T(128)}, f32[128]{0:T(128)S(1)}, u32[]{:S(2)}) copy-start(f32[128]{0:T(128)S(1)} %broadcast_multiply_fusion.2) | copy-start | bytes 1540
  32.8 258.7 %copy-start.35 = (f32[128]{0:T(128)}, f32[128]{0:T(128)S(1)}, u32[]{:S(2)}) copy-start(f32[128]{0:T(128)S(1)} %fusion.110) | copy-start | bytes 1540
  291.6 7.0 copy-start.39
  292.7 67.6 %all-gather.9.cloned.1.call-start = ((), (), s32[]{:S(2)}) async-start(), calls=%async_computation.11 | async-start | bytes 3686400 | tf_op jit(solution)/shard_map/all_gather | solution.py:72
  293.4 232.4 %all-gather.13.cloned.1.call-start = ((), (), s32[]{:S(2)}) async-start(), calls=%async_computation.13 | async-start | bytes 6656000 | tf_op jit(solution)/shard_map/all_gather | solution.py:58
  294.7 22.1 %all-to-all-start = ((bf16[400,4,3]{0,2,1:T(4,128)(2,1)}), bf16[400,4,3]{0,2,1:T(4,128)(2,1)S(1)}, u32[]{:S(2)}, u32[]{:S(2)}) async-start(bf16[400,4,3]{0,2,1:T(4,128)(2,1)} %tile.2), calls=%async_computation | async-start | bytes 32768 | tf_op jit(solution)/shard_map/all_to_all | solution.py:127
  297.9 267.0 %all-gather.17.cloned.1.call-start = ((), (), s32[]{:S(2)}) async-start(), calls=%async_computation.15 | async-start | bytes 2048000 | tf_op jit(solution)/shard_map/all_gather | solution.py:135
  316.8 256.0 %all-to-all-start.1 = ((bf16[400,4,1600]{2,0,1:T(8,128)(2,1)}), bf16[400,4,1600]{2,0,1:T(8,128)(2,1)}, u32[]{:S(2)}, u32[]{:S(2)}) async-start(bf16[400,4,1600]{2,0,1:T(8,128)(2,1)} %copy.78), calls=%async_computation.1 | async-start | bytes 10649600 | tf_op jit(solution)/shard_map/all_to_all | solution.py:126
  321.9 282.0 %all-gather.15.cloned.1.call-start = ((), (), s32[]{:S(2)}) async-start(), calls=%async_computation.14 | async-start | bytes 2048000 | tf_op jit(solution)/shard_map/all_gather | solution.py:134
  525.8 7.2 copy-start.37
  532.9 130.0 %reduce-scatter.21.cloned.1.call-start = ((), (), s32[]{:S(2)}) async-start(), calls=%async_computation.19 | async-start | bytes 2129920
  627.1 153.6 %reduce-scatter.25.cloned.1.call-start = ((), (), s32[]{:S(2)}) async-start(), calls=%async_computation.21 | async-start | bytes 3833856
  675.8 5.2 copy-start
  692.3 6.0 copy-start.13
  700.1 5.2 copy-start
  712.0 4.8 copy-start.15
  716.8 6.0 copy-start.13
  734.3 97.8 %reduce-scatter.23.cloned.1.call-start = ((), (), s32[]{:S(2)}) async-start(), calls=%async_computation.20 | async-start | bytes 3833856
  744.0 323.8 %reduce-scatter.17.cloned.1.call-start = ((), (), s32[]{:S(2)}) async-start(), calls=%async_computation.17 | async-start | bytes 6656000 | tf_op jit(solution)/shard_map/reduce_scatter | solution.py:276
  749.1 84.2 %copy-start.8 = (bf16[128,1600]{0,1:T(8,128)(2,1)S(1)}, bf16[128,1600]{0,1:T(8,128)(2,1)}, u32[]{:S(2)}) copy-start(bf16[128,1600]{0,1:T(8,128)(2,1)} %param.22) | copy-start | bytes 1228804
  749.1 84.2 %copy-start.29 = (f32[1600]{0:T(1024)S(1)}, f32[1600]{0:T(1024)}, u32[]{:S(2)}) copy-start(f32[1600]{0:T(1024)} %copy-done.28) | copy-start | bytes 19204
  749.1 84.2 %copy-start.31 = (f32[1600]{0:T(1024)S(1)}, f32[1600]{0:T(1024)}, u32[]{:S(2)}) copy-start(f32[1600]{0:T(1024)} %copy-done.30) | copy-start | bytes 19204
  749.1 84.2 %copy-start.34 = (f32[128]{0:T(128)S(1)}, f32[128]{0:T(128)}, u32[]{:S(2)}) copy-start(f32[128]{0:T(128)} %copy-done.33) | copy-start | bytes 1540
  749.1 84.2 %copy-start.36 = (f32[128]{0:T(128)S(1)}, f32[128]{0:T(128)}, u32[]{:S(2)}) copy-start(f32[128]{0:T(128)} %copy-done.35) | copy-start | bytes 1540
  749.1 546.8 %reduce-scatter.15.cloned.1.call-start = ((), (), s32[]{:S(2)}) async-start(), calls=%async_computation.16 | async-start | bytes 19456000 | tf_op jit(solution)/shard_map/reduce_scatter | solution.py:267
  750.5 91.3 %copy-start.21 = (bf16[128,25,64]{0,2,1:T(8,128)(2,1)}, bf16[128,25,64]{0,2,1:T(8,128)(2,1)S(1)}, u32[]{:S(2)}) copy-start(bf16[128,25,64]{0,2,1:T(8,128)(2,1)S(1)} %get-tuple-element.465) | copy-start | bytes 1228804
  781.9 59.9 %copy-start.22 = (bf16[128,1600]{0,1:T(8,128)(2,1)}, bf16[128,1600]{0,1:T(8,128)(2,1)S(1)}, u32[]{:S(2)}) copy-start(bf16[128,1600]{0,1:T(8,128)(2,1)S(1)} %copy.96) | copy-start | bytes 1228804
  833.3 8.5 copy-start.23
  849.6 201.4 %all-to-all-start.3 = ((bf16[4,400,1600]{2,1,0:T(8,128)(2,1)}), bf16[4,400,1600]{2,1,0:T(8,128)(2,1)}, u32[]{:S(2)}, u32[]{:S(2)}) async-start(bf16[4,400,1600]{2,1,0:T(8,128)(2,1)} %bitcast.213), calls=%async_computation.5 | async-start | bytes 10649600 | tf_op jit(solution)/shard_map/all_to_all | solution.py:178
  854.7 480.5 %reduce-scatter.19.cloned.1.call-start = ((), (), s32[]{:S(2)}) async-start(), calls=%async_computation.18 | async-start | bytes 2129920
  866.7 678.8 %all-reduce.16.cloned.1.call-start = ((), (), s32[]{:S(2)}) async-start(), calls=%async_computation.22 | async-start | bytes 31334400 | tf_op jit(solution)/shard_map/psum | solution.py:286
  1296.0 40.5 %copy-start.19 = (bf16[128,1600]{1,0:T(8,128)(2,1)S(1)}, bf16[128,1600]{1,0:T(8,128)(2,1)}, u32[]{:S(2)}) copy-start(bf16[128,1600]{1,0:T(8,128)(2,1)} %reduce-scatter.25.cloned.1.call-done) | copy-start | bytes 1228804
  1297.9 38.6 %all-to-all-start.2 = ((bf16[4,400,2]{1,2,0:T(2,128)(2,1)}), bf16[4,400,2]{1,2,0:T(2,128)(2,1)S(1)}, u32[]{:S(2)}, u32[]{:S(2)}) async-start(bf16[4,400,2]{1,2,0:T(2,128)(2,1)} %copy.83), calls=%async_computation.4 | async-start | bytes 16384 | tf_op jit(solution)/shard_map/all_to_all | solution.py:181
  1336.6 9.4 copy-start.50
  1336.6 27.3 %copy-start.38 = (bf16[1600]{0:T(1024)(128)(2,1)S(1)}, bf16[1600]{0:T(1024)(128)(2,1)}, u32[]{:S(2)}) copy-start(bf16[1600]{0:T(1024)(128)(2,1)} %get-tuple-element.460) | copy-start | bytes 9604
  1336.6 56.7 %copy-start.5 = (f32[128,1600]{0,1:T(8,128)S(1)}, f32[128,1600]{0,1:T(8,128)}, u32[]{:S(2)}) copy-start(f32[128,1600]{0,1:T(8,128)} %copy-done.4) | copy-start | bytes 2457604
  1336.6 56.7 %copy-start.9 = (bf16[128,1600]{0,1:T(8,128)(2,1)S(1)}, bf16[128,1600]{0,1:T(8,128)(2,1)}, u32[]{:S(2)}) copy-start(bf16[128,1600]{0,1:T(8,128)(2,1)} %copy.92) | copy-start | bytes 1228804
  1336.7 56.7 %copy-start.11 = (bf16[128,1600]{0,1:T(8,128)(2,1)S(1)}, bf16[128,1600]{0,1:T(8,128)(2,1)}, u32[]{:S(2)}) copy-start(bf16[128,1600]{0,1:T(8,128)(2,1)} %param.37) | copy-start | bytes 1228804
  1336.7 56.6 %copy-start.32 = (f32[1600]{0:T(1024)S(1)}, f32[1600]{0:T(1024)}, u32[]{:S(2)}) copy-start(f32[1600]{0:T(1024)} %get-tuple-element.378) | copy-start | bytes 19204
  1545.5 7.6 slice-start.2
  1545.5 6.0 copy-start.26
  1545.5 7.6 slice-start.3
  1551.5 6.4 slice-start
  (34 other events, 89.3 us)
Sparse Core Ops, SparseCore 0:
  9.6 269.6 all-gather.6
  292.8 31.6 all-gather.10
  326.9 33.2 all-gather.8
  361.7 164.0 all-gather.12
  527.2 37.6 all-gather.16
  566.9 36.9 all-gather.14
  627.2 35.6 reduce-scatter.20
  734.4 46.2 reduce-scatter.24
  784.7 47.3 reduce-scatter.22
  834.8 164.3 reduce-scatter.16
  1001.5 294.3 reduce-scatter.14
  1298.7 36.4 reduce-scatter.18
  1339.8 205.6 all-reduce.15
where the time goes:
time: 1580 us; the launch traced here: 1570 us
  waiting for transfers between devices  1150 us (73%)
  matrix products  151 us (10%)
  local copies, waits for them, and re-layouts  113 us (7%)
  blocking collectives  62.2 us (4%)
  other arithmetic  45.8 us (3%)
  starting transfers between devices  18.1 us (1%)
  between operations  16.5 us (1%)
    all_gather x1, waiting for transfers between devices, body(): lax.all_gather(qkv_weight, 'fsdp', axis=0, tiled=True)  247 us
    reduce_scatter x1, waiting for transfers between devices, body(): lax.psum_scatter(grad_qkv_w.astype(jnp.bfloat16), 'fsdp', scatter_dimensi...  228 us
    all_to_all x1, waiting for transfers between devices, body(): lax.all_to_all(grad_fc_cols.astype(jnp.bfloat16), 'fsdp', split_axis=0, c...  176 us
    unnamed x17, waiting for transfers between devices  152 us
    psum x1, waiting for transfers between devices, body(): lax.psum(owned_qkv.astype(jnp.bfloat16), 'ctx').astype(jnp.float32)  150 us
    all_gather x1, waiting for transfers between devices, body(): lax.all_gather(proj_weight, 'fsdp', axis=0, tiled=True)  129 us
    unnamed x127, local copies, waits for them, and re-layouts  40.2 us
    unnamed x2, blocking collectives  38 us
  transfers between devices with their start and end apart: 17, of which 13 were waited for; matrix products, arithmetic and copies ran while one was open for 10% of the time, Pallas kernels for 0%

commit v1 on v0

--- a/solution.py
+++ b/solution.py
@@ -5,6 +5,18 @@
 from jax.sharding import PartitionSpec as P
 
 HEADS = 25
+
+
+def doubled_up(x, axis, dim):
+    ways, here = (lax.axis_size(axis), lax.axis_index(axis))
+    grown, reach = (x, 1)
+    while reach < ways:
+        theirs = lax.ppermute(grown, axis, [(d, d ^ reach) for d in range(ways)])
+        mine_first = jnp.concatenate([grown, theirs], axis=dim)
+        theirs_first = jnp.concatenate([theirs, grown], axis=dim)
+        grown = jnp.where(here & reach == 0, mine_first, theirs_first)
+        reach = 2 * reach
+    return grown
 
 
 def layer_norm(values, gain_vec, shift_vec):
@@ -55,7 +67,7 @@
         lax.all_gather(qkv_weight, "fsdp", axis=0, tiled=True),
         lax.all_gather(query_bias, "fsdp", axis=0, tiled=True),
         lax.all_gather(value_bias, "fsdp", axis=0, tiled=True),
-        lax.all_gather(proj_weight, "fsdp", axis=0, tiled=True),
+        doubled_up(proj_weight, "fsdp", 0),
         lax.all_gather(proj_bias, "fsdp", axis=0, tiled=True),
     )
     inputs = tokens.astype(jnp.float32)

time: 1580 us -> 1610 us (1.019)
  waiting for transfers between devices: 1150 us -> 1190 us
    ppermute x0 -> x2, waiting for transfers between devices: none -> 195 us  [doubled_up(): theirs = lax.ppermute(grown, axis, [(d, d ^ reach) for d in range(ways)])]
    all_gather x1 -> x0, waiting for transfers between devices: 129 us -> none  [body(): lax.all_gather(proj_weight, 'fsdp', axis=0, tiled=True)]
    all_gather x1, waiting for transfers between devices: 31.9 us -> 0.02 us  [body(): lax.all_gather(cotangent, 'fsdp', axis=0, tiled=True)]
    unnamed x127 -> x131, local copies, waits for them, and re-layouts: 40.2 us -> 39.7 us
    unnamed x17 -> x16, waiting for transfers between devices: 152 us -> 152 us
  transfers between devices with their start and end apart: 17 -> 18, of which waited for: 13 -> 11; matrix products, arithmetic and copies ran while one was open for 10% -> 10% of each run, Pallas kernels for 0% -> 0%
where the time goes in v1:
time: 1610 us; the launch traced here: 1600 us
  waiting for transfers between devices  1190 us (74%)
  matrix products  155 us (10%)
  local copies, waits for them, and re-layouts  113 us (7%)
  blocking collectives  62.3 us (4%)
  other arithmetic  47.6 us (3%)
  starting transfers between devices  20.4 us (1%)
  between operations  16.6 us (1%)
    all_gather x1, waiting for transfers between devices, body(): lax.all_gather(qkv_weight, 'fsdp', axis=0, tiled=True)  247 us
    reduce_scatter x1, waiting for transfers between devices, body(): lax.psum_scatter(grad_qkv_w.astype(jnp.bfloat16), 'fsdp', scatter_dimensi...  228 us
    ppermute x2, waiting for transfers between devices, doubled_up(): theirs = lax.ppermute(grown, axis, [(d, d ^ reach) for d in range(ways)])  195 us
    all_to_all x1, waiting for transfers between devices, body(): lax.all_to_all(grad_fc_cols.astype(jnp.bfloat16), 'fsdp', split_axis=0, c...  176 us
    unnamed x16, waiting for transfers between devices  152 us
    psum x1, waiting for transfers between devices, body(): lax.psum(owned_qkv.astype(jnp.bfloat16), 'ctx').astype(jnp.float32)  150 us
    unnamed x131, local copies, waits for them, and re-layouts  39.7 us
    unnamed x2, blocking collectives  38 us
  transfers between devices with their start and end apart: 18, of which 11 were waited for; matrix products, arithmetic and copies ran while one was open for 10% of the time, Pallas kernels for 0%

profile of v1, /device:TPU:0, one launch (start us, length us, event | category | flops | bytes accessed | tf_op | source)
XLA Modules:
  0.0 1602.5 jit_solution(6057637392929540786)
XLA Ops:
  10.6 21.1 %all-reduce.13 = (bf16[1600]{0:T(1024)(128)(2,1)S(1)}, bf16[1600]{0:T(1024)(128)(2,1)S(1)}, bf16[1600]{0:T(1024)(128)(2,1)S(1)}, bf16[1600]{0:T(1024)(128)(2,1)S(1)}, bf16[1600]{0:T(1024)(128)(2,1)S(1)}) all-reduce(bf16[1600]{0:T(1024)(128)(2,1)S(1)} %dynamic-update-slice.2, ...), channel_id=1, replica_groups=mesh['ctx'=8,'fsdp'=4] {'fsdp'}, use_global_device_ids=true, to_apply=%add.2 | all-reduce | flops 8000 | bytes 32000
  32.8 246.5 %all-gather.6.cloned.1.call-done = bf16[1600,4800]{1,0:T(8,128)(2,1)} async-done(((bf16[400,4800]{1,0:T(8,128)(2,1)}), bf16[1600,4800]{1,0:T(8,128)(2,1)}) %all-gather.6.cloned.1.call-update) | async-done | bytes 15360016 | tf_op jit(solution)/shard_map/all_gather | solution.py:67
  279.4 12.1 fusion.80
  298.5 11.7 all_to_all.51
  310.2 6.0 copy.78
  316.4 8.4 all-to-all-done
  324.9 5.1 all-to-all-start.1
  336.1 8.5 reshape.304
  347.2 19.6 %while.39 = (s32[]{:T(128)}, f32[25,128]{1,0:T(8,128)S(1)}, f32[25,128]{1,0:T(8,128)S(1)}, s32[2,512]{1,0:T(2,128)S(1)}, bf16[2,512,25,64]{1,3,2,0:T(8,128)(2,1)...) while((s32[]{:T(128)}, f32[25,128]{1,0:T(8,128)S(1)}, ...), condition=%wide.region_5.6_spmd.clone, body=%wide.region_2.5_spmd.clone.sunk | while | flops 221265664 | bytes 15526528 | solution.py:110
  347.5 5.2 fusion.175
  357.4 5.2 fusion.175
  366.9 8.5 reshape.303
  379.8 10.8 while.40
  380.1 4.7 fusion.181
  385.2 5.0 fusion.181
  391.8 195.5 %collective-permute-done.1 = bf16[800,1600]{1,0:T(8,128)(2,1)} collective-permute-done((bf16[800,1600]{1,0:T(8,128)(2,1)}, bf16[800,1600]{1,0:T(8,128)(2,1)}, u32[]{:S(2)}, u32[]{:S(2)}) %collective-permute-start.1) | collective-permute-done | bytes 2560032 | tf_op jit(solution)/shard_map/ppermute | solution.py:14
  587.3 7.1 fusion.127
  596.7 7.9 fusion.128
  604.6 30.0 %all-gather.12.cloned.1.call-done = bf16[512,1600]{0,1:T(8,128)(2,1)} async-done(((bf16[128,1600]{0,1:T(8,128)(2,1)}), bf16[512,1600]{0,1:T(8,128)(2,1)}) %all-gather.12.cloned.1.call-update) | async-done | bytes 1638416 | tf_op jit(solution)/shard_map/all_gather | solution.py:146
  634.6 11.7 fusion.120
  647.4 6.9 convolution_convert_fusion.4
  657.9 35.8 %reduce-scatter.21.cloned.1.call-done = bf16[128,1600]{1,0:T(8,128)(2,1)} async-done(((bf16[512,1600]{1,0:T(8,128)(2,1)}), bf16[128,1600]{1,0:T(8,128)(2,1)}) %reduce-scatter.21.cloned.1.call-update) | async-done | bytes 409616
  701.1 6.4 convolution_convert_fusion.6
  708.3 48.8 %while.41 = (s32[]{:T(128)}, f32[128,25,64]{0,2,1:T(8,128)}, bf16[2,512,25,64]{1,3,2,0:T(8,128)(2,1)}, bf16[2,512,25,64]{1,3,2,0:T(8,128)(2,1)}, bf16[2,512,25,6...) while((s32[]{:T(128)}, f32[128,25,64]{0,2,1:T(8,128)}, ...), condition=%wide.region_16.17_spmd.clone, body=%wide.region_15.16_spmd.clone.sunk | while | flops 1068712064 | bytes 150980000 | solution.py:243
  708.3 5.1 fusion.192
  713.8 6.4 fusion.193
  732.5 5.1 fusion.192
  737.9 6.4 fusion.193
  757.1 5.3 copy.82
  783.1 30.1 %reduce-scatter.25.cloned.1.call-done = bf16[128,1600]{1,0:T(8,128)(2,1)} async-done(((bf16[1024,1600]{1,0:T(8,128)(2,1)}), bf16[128,1600]{1,0:T(8,128)(2,1)}) %reduce-scatter.25.cloned.1.call-update) | async-done | bytes 409616
  814.5 50.1 %reduce-scatter.23.cloned.1.call-done = bf16[128,1600]{1,0:T(8,128)(2,1)} async-done(((bf16[1024,1600]{1,0:T(8,128)(2,1)}), bf16[128,1600]{1,0:T(8,128)(2,1)}) %reduce-scatter.23.cloned.1.call-update) | async-done | bytes 409616
  865.9 8.9 convolution_convert_fusion
  876.3 6.3 convolution_convert_fusion.2
  882.6 5.1 all-to-all-start.3
  887.7 8.0 convolution_convert_fusion.5
  899.7 8.1 convolution_convert_fusion.1
  907.8 176.2 %all-to-all-done.3 = bf16[4,400,1600]{2,1,0:T(8,128)(2,1)} async-done(((bf16[4,400,1600]{2,1,0:T(8,128)(2,1)}), bf16[4,400,1600]{2,1,0:T(8,128)(2,1)}, u32[]{:S(2)}, u32[]{:S(2)}) %all-to-all-start.3) | async-done | bytes 5120032 | tf_op jit(solution)/shard_map/all_to_all | solution.py:190
  1084.0 6.9 copy.84
  1091.0 9.8 all_to_all.59
  1100.8 227.9 %reduce-scatter.15.cloned.1.call-done = bf16[400,4800]{1,0:T(8,128)(2,1)} async-done(((bf16[1600,4800]{1,0:T(8,128)(2,1)}), bf16[400,4800]{1,0:T(8,128)(2,1)}) %reduce-scatter.15.cloned.1.call-update) | async-done | bytes 3840016 | tf_op jit(solution)/shard_map/reduce_scatter | solution.py:279
  1334.3 33.8 %reduce-scatter.19.cloned.1.call-done = bf16[128,1600]{1,0:T(8,128)(2,1)} async-done(((bf16[512,1600]{1,0:T(8,128)(2,1)}), bf16[128,1600]{1,0:T(8,128)(2,1)}) %reduce-scatter.19.cloned.1.call-update) | async-done | bytes 409616
  1369.6 9.3 fusion.119
  1379.5 16.9 %all-reduce.12 = (bf16[1600]{0:T(1024)(128)(2,1)S(1)}, bf16[1600]{0:T(1024)(128)(2,1)S(1)}, bf16[1600]{0:T(1024)(128)(2,1)S(1)}, bf16[1600]{0:T(1024)(128)(2,1)S(1)}, bf16[1600]{0:T(1024)(128)(2,1)S(1)}) all-reduce(bf16[1600]{0:T(1024)(128)(2,1)S(1)} %get-tuple-element.374, ...), channel_id=6, replica_groups=mesh['ctx'=8,'fsdp'=4] {'fsdp'}, use_global_device_ids=true, to_apply=%region_22.23.clone | all-reduce | flops 8000 | bytes 32000
  1396.8 24.2 %all-reduce.10 = (bf16[400]{0:T(512)(128)(2,1)S(1)}, bf16[400]{0:T(512)(128)(2,1)S(1)}, bf16[400]{0:T(512)(128)(2,1)S(1)}, bf16[400]{0:T(512)(128)(2,1)S(1)}, bf...) all-reduce(bf16[400]{0:T(512)(128)(2,1)S(1)} %dynamic-slice.6, ...), channel_id=1, replica_groups=mesh['ctx'=8,'fsdp'=4] {'ctx'}, use_global_device_ids=true, to_apply=%region_23.24 | all-reduce | flops 4800 | bytes 19200 | tf_op jit(solution)/shard_map/psum | solution.py:296
  1428.2 150.0 %all-reduce.16.cloned.1.call-done = (bf16[400,4800]{1,0:T(8,128)(2,1)}, bf16[400,1600]{1,0:T(8,128)(2,1)}, bf16[400,6400]{1,0:T(8,128)(2,1)}, bf16[1600,1600]{1,0:T(8,128)(2,1)}) async-done(((bf16[400,4800]{1,0:T(8,128)(2,1)}, bf16[400,1600]{1,0:T(8,128)(2,1)}, bf16[400,6400]{1,0:T(8,128)(2,1)}, bf16[1600,1600]{1,0:T(8,128)(2,1)}), (bf16[400,4800]{1,0:T(8,128)(2,1)}, bf16[400,1600]{1,0:T(8,128)(2,1)}, ...) | async-done | bytes 15360016 | tf_op jit(solution)/shard_map/psum | solution.py:298
  1578.3 6.0 convert_element_type.266
  1585.9 4.7 convert_element_type.278
  1590.6 4.8 convert_element_type.281
  (313 shorter events, 119.9 us)
Async XLA Ops:
  7.2 24.6 %copy-start.7 = (bf16[128,1600]{0,1:T(8,128)(2,1)S(1)}, bf16[128,1600]{0,1:T(8,128)(2,1)}, u32[]{:S(2)}) copy-start(bf16[128,1600]{0,1:T(8,128)(2,1)} %param.22) | copy-start | bytes 1228804
  7.3 272.1 %all-gather.6.cloned.1.call-start = ((), (), s32[]{:S(2)}) async-start(), calls=%async_computation.10 | async-start | bytes 19456000 | tf_op jit(solution)/shard_map/all_gather | solution.py:67
  8.0 328.1 %all-gather.10.cloned.1.call-start = ((), (), s32[]{:S(2)}) async-start(), calls=%async_computation.12 | async-start | bytes 3686400 | tf_op jit(solution)/shard_map/all_gather | solution.py:83
  31.7 247.7 %copy-start.30 = (f32[1600]{0:T(1024)}, f32[1600]{0:T(1024)S(1)}, u32[]{:S(2)}) copy-start(f32[1600]{0:T(1024)S(1)} %convert_element_type.230) | copy-start | bytes 19204
  31.8 247.5 %copy-start.32 = (f32[1600]{0:T(1024)}, f32[1600]{0:T(1024)S(1)}, u32[]{:S(2)}) copy-start(f32[1600]{0:T(1024)S(1)} %convert_element_type.231) | copy-start | bytes 19204
  32.1 247.3 %copy-start.35 = (f32[128]{0:T(128)}, f32[128]{0:T(128)S(1)}, u32[]{:S(2)}) copy-start(f32[128]{0:T(128)S(1)} %broadcast_multiply_fusion.2) | copy-start | bytes 1540
  32.8 246.5 %copy-start.37 = (f32[128]{0:T(128)}, f32[128]{0:T(128)S(1)}, u32[]{:S(2)}) copy-start(f32[128]{0:T(128)S(1)} %fusion.110) | copy-start | bytes 1540
  291.6 6.5 copy-start.41
  292.7 74.2 %all-gather.8.cloned.1.call-start = ((), (), s32[]{:S(2)}) async-start(), calls=%async_computation.11 | async-start | bytes 3686400 | tf_op jit(solution)/shard_map/all_gather | solution.py:84
  293.4 37.3 %collective-permute-start = (bf16[400,1600]{1,0:T(8,128)(2,1)S(1)}, bf16[400,1600]{1,0:T(8,128)(2,1)S(1)}, u32[]{:S(2)}, u32[]{:S(2)}) collective-permute-start(bf16[400,1600]{1,0:T(8,128)(2,1)S(1)} %copy-done.28), channel_id=1, source_target_pairs={{0,1},{1,0},{2,3},{3,2},{4,5},{5,4},{6,7},{7,6},{8,9},{9,8},{10,11... | collective-permute-start | bytes 3840008 | tf_op jit(solution)/shard_map/ppermute | solution.py:14
  294.2 30.7 %all-to-all-start = ((bf16[400,4,3]{0,2,1:T(4,128)(2,1)}), bf16[400,4,3]{0,2,1:T(4,128)(2,1)S(1)}, u32[]{:S(2)}, u32[]{:S(2)}) async-start(bf16[400,4,3]{0,2,1:T(4,128)(2,1)} %tile.2), calls=%async_computation | async-start | bytes 32768 | tf_op jit(solution)/shard_map/all_to_all | solution.py:139
  297.5 299.2 %all-gather.14.cloned.1.call-start = ((), (), s32[]{:S(2)}) async-start(), calls=%async_computation.14 | async-start | bytes 2048000 | tf_op jit(solution)/shard_map/all_gather | solution.py:147
  324.9 279.7 %all-to-all-start.1 = ((bf16[400,4,1600]{2,0,1:T(8,128)(2,1)}), bf16[400,4,1600]{2,0,1:T(8,128)(2,1)}, u32[]{:S(2)}, u32[]{:S(2)}) async-start(bf16[400,4,1600]{2,0,1:T(8,128)(2,1)} %copy.78), calls=%async_computation.1 | async-start | bytes 10649600 | tf_op jit(solution)/shard_map/all_to_all | solution.py:138
  329.9 304.6 %all-gather.12.cloned.1.call-start = ((), (), s32[]{:S(2)}) async-start(), calls=%async_computation.13 | async-start | bytes 2048000 | tf_op jit(solution)/shard_map/all_gather | solution.py:146
  333.2 254.1 %collective-permute-start.1 = (bf16[800,1600]{1,0:T(8,128)(2,1)}, bf16[800,1600]{1,0:T(8,128)(2,1)}, u32[]{:S(2)}, u32[]{:S(2)}) collective-permute-start(bf16[800,1600]{1,0:T(8,128)(2,1)} %maximum_select_fusion.1), channel_id=1, source_target_pairs={{0,2},{1,3},{2,0},{3,1},{4,6},{5,7},{6,4},{7,5},{8,10},{9,11},{10,... | collective-permute-start | bytes 7680008 | tf_op jit(solution)/shard_map/ppermute | solution.py:14
  391.8 202.6 %copy-start.17 = (bf16[128,25,64]{0,2,1:T(8,128)(2,1)}, bf16[128,25,64]{0,2,1:T(8,128)(2,1)S(1)}, u32[]{:S(2)}) copy-start(bf16[128,25,64]{0,2,1:T(8,128)(2,1)S(1)} %convert_element_type.234) | copy-start | bytes 1228804
  587.3 9.3 copy-start.39
  596.6 97.1 %reduce-scatter.21.cloned.1.call-start = ((), (), s32[]{:S(2)}) async-start(), calls=%async_computation.18 | async-start | bytes 2129920
  657.8 155.4 %reduce-scatter.25.cloned.1.call-start = ((), (), s32[]{:S(2)}) async-start(), calls=%async_computation.20 | async-start | bytes 3833856
  701.1 6.4 copy-start.25
  701.1 6.4 copy-start.16
  724.7 6.0 copy-start.12
  749.1 6.0 copy-start.12
  766.8 97.8 %reduce-scatter.23.cloned.1.call-start = ((), (), s32[]{:S(2)}) async-start(), calls=%async_computation.19 | async-start | bytes 3833856
  776.5 324.3 %reduce-scatter.17.cloned.1.call-start = ((), (), s32[]{:S(2)}) async-start(), calls=%async_computation.16 | async-start | bytes 6656000 | tf_op jit(solution)/shard_map/reduce_scatter | solution.py:288
  781.6 84.2 %copy-start.8 = (bf16[128,1600]{0,1:T(8,128)(2,1)S(1)}, bf16[128,1600]{0,1:T(8,128)(2,1)}, u32[]{:S(2)}) copy-start(bf16[128,1600]{0,1:T(8,128)(2,1)} %param.22) | copy-start | bytes 1228804
  781.6 84.2 %copy-start.31 = (f32[1600]{0:T(1024)S(1)}, f32[1600]{0:T(1024)}, u32[]{:S(2)}) copy-start(f32[1600]{0:T(1024)} %copy-done.30) | copy-start | bytes 19204
  781.6 84.3 %copy-start.33 = (f32[1600]{0:T(1024)S(1)}, f32[1600]{0:T(1024)}, u32[]{:S(2)}) copy-start(f32[1600]{0:T(1024)} %copy-done.32) | copy-start | bytes 19204
  781.7 84.3 %copy-start.36 = (f32[128]{0:T(128)S(1)}, f32[128]{0:T(128)}, u32[]{:S(2)}) copy-start(f32[128]{0:T(128)} %copy-done.35) | copy-start | bytes 1540
  781.7 84.3 %copy-start.38 = (f32[128]{0:T(128)S(1)}, f32[128]{0:T(128)}, u32[]{:S(2)}) copy-start(f32[128]{0:T(128)} %copy-done.37) | copy-start | bytes 1540
  781.7 547.0 %reduce-scatter.15.cloned.1.call-start = ((), (), s32[]{:S(2)}) async-start(), calls=%async_computation.15 | async-start | bytes 19456000 | tf_op jit(solution)/shard_map/reduce_scatter | solution.py:279
  783.1 91.8 %copy-start.22 = (bf16[128,25,64]{0,2,1:T(8,128)(2,1)}, bf16[128,25,64]{0,2,1:T(8,128)(2,1)S(1)}, u32[]{:S(2)}) copy-start(bf16[128,25,64]{0,2,1:T(8,128)(2,1)S(1)} %get-tuple-element.465) | copy-start | bytes 1228804
  814.5 60.4 %copy-start.23 = (bf16[128,1600]{0,1:T(8,128)(2,1)}, bf16[128,1600]{0,1:T(8,128)(2,1)S(1)}, u32[]{:S(2)}) copy-start(bf16[128,1600]{0,1:T(8,128)(2,1)S(1)} %copy.96) | copy-start | bytes 1228804
  865.9 9.0 copy-start.24
  882.6 201.4 %all-to-all-start.3 = ((bf16[4,400,1600]{2,1,0:T(8,128)(2,1)}), bf16[4,400,1600]{2,1,0:T(8,128)(2,1)}, u32[]{:S(2)}, u32[]{:S(2)}) async-start(bf16[4,400,1600]{2,1,0:T(8,128)(2,1)} %bitcast.209), calls=%async_computation.5 | async-start | bytes 10649600 | tf_op jit(solution)/shard_map/all_to_all | solution.py:190
  887.7 480.4 %reduce-scatter.19.cloned.1.call-start = ((), (), s32[]{:S(2)}) async-start(), calls=%async_computation.17 | async-start | bytes 2129920
  899.5 678.8 %all-reduce.16.cloned.1.call-start = ((), (), s32[]{:S(2)}) async-start(), calls=%async_computation.21 | async-start | bytes 31334400 | tf_op jit(solution)/shard_map/psum | solution.py:298
  1328.7 40.7 %copy-start.20 = (bf16[128,1600]{1,0:T(8,128)(2,1)S(1)}, bf16[128,1600]{1,0:T(8,128)(2,1)}, u32[]{:S(2)}) copy-start(bf16[128,1600]{1,0:T(8,128)(2,1)} %reduce-scatter.25.cloned.1.call-done) | copy-start | bytes 1228804
  1330.6 38.8 %all-to-all-start.2 = ((bf16[4,400,2]{1,2,0:T(2,128)(2,1)}), bf16[4,400,2]{1,2,0:T(2,128)(2,1)S(1)}, u32[]{:S(2)}, u32[]{:S(2)}) async-start(bf16[4,400,2]{1,2,0:T(2,128)(2,1)} %copy.83), calls=%async_computation.4 | async-start | bytes 16384 | tf_op jit(solution)/shard_map/all_to_all | solution.py:193
  1369.5 9.4 copy-start.52
  1369.5 27.3 %copy-start.40 = (bf16[1600]{0:T(1024)(128)(2,1)S(1)}, bf16[1600]{0:T(1024)(128)(2,1)}, u32[]{:S(2)}) copy-start(bf16[1600]{0:T(1024)(128)(2,1)} %get-tuple-element.460) | copy-start | bytes 9604
  1369.6 56.8 %copy-start.5 = (f32[128,1600]{0,1:T(8,128)S(1)}, f32[128,1600]{0,1:T(8,128)}, u32[]{:S(2)}) copy-start(f32[128,1600]{0,1:T(8,128)} %copy-done.4) | copy-start | bytes 2457604
  1369.6 56.8 %copy-start.9 = (bf16[128,1600]{0,1:T(8,128)(2,1)S(1)}, bf16[128,1600]{0,1:T(8,128)(2,1)}, u32[]{:S(2)}) copy-start(bf16[128,1600]{0,1:T(8,128)(2,1)} %copy.92) | copy-start | bytes 1228804
  1369.6 56.7 %copy-start.10 = (bf16[128,1600]{0,1:T(8,128)(2,1)S(1)}, bf16[128,1600]{0,1:T(8,128)(2,1)}, u32[]{:S(2)}) copy-start(bf16[128,1600]{0,1:T(8,128)(2,1)} %param.37) | copy-start | bytes 1228804
  1369.6 56.7 %copy-start.34 = (f32[1600]{0:T(1024)S(1)}, f32[1600]{0:T(1024)}, u32[]{:S(2)}) copy-start(f32[1600]{0:T(1024)} %get-tuple-element.378) | copy-start | bytes 19204
  1578.3 7.6 slice-start.2
  1578.3 7.6 slice-start.3
  1584.2 6.4 slice-start
  (37 other events, 102.0 us)
Sparse Core Ops, SparseCore 0:
  9.6 269.6 all-gather.5
  292.8 31.6 all-gather.9
  326.9 33.2 all-gather.7
  361.6 154.0 all-gather.13
  596.7 37.7 all-gather.11
  658.0 35.6 reduce-scatter.20
  766.9 46.2 reduce-scatter.24
  817.3 47.3 reduce-scatter.22
  867.5 164.1 reduce-scatter.16
  1034.0 294.6 reduce-scatter.14
  1331.6 36.5 reduce-scatter.18
  1372.6 205.6 all-reduce.15
